TPU v7x, 256 devices: a whole 4x4x8 slice. The times are simulated.
256 devices in a mesh: tok: 8 (over x, core), col: 32 (over y, z).
Axes of the slice: x: 4, y: 4, z: 8, core: 2. Of those that a mesh axis runs over, the one named last changes fastest.
Arguments:
- hidden_in: bfloat16 [2048, 36864], P('tok', 'col'), may hold values from -6 to 6
- down_weight: bfloat16 [4608, 36864], P('col', 'tok'), may hold values from -0.046875 to 0.046875
- keep_mask: int32 [4608, 36864], P('col', 'tok'), may hold values 0 or 1
Outputs:
- layer_out: bfloat16 [2048, 4608], P(('tok', 'col'))
- hessian: float32 [4608, 4608], P('col', 'tok')
All inputs are finite; a program needn't handle non-finite values. No bound on the sum of `keep_mask` on one device may be relied on, other than what follows from the above.
Results may differ from a plain program's by a relative error of at most 0.012.
Values may be sent and summed in bfloat16 or wider, within the bound.
A program may use at most 128 MiB of HBM per device.

v0:
```python
import jax
import jax.numpy as jnp
from jax import lax
from jax.sharding import PartitionSpec as P


def laid_out(pieces, dim):
    lengths = list(pieces.shape[1:])
    lengths[dim] *= pieces.shape[0]
    return jnp.moveaxis(pieces, 0, dim).reshape(lengths)


def from_everyone(x, axis):
    size = lax.axis_size(axis)
    return lax.all_to_all(jnp.broadcast_to(x[None], (size, *x.shape)), axis, 0, 0, tiled=True)


def gathered_copies(x, axis, dim):
    return laid_out(from_everyone(x, axis), dim)


def split_up(x, dim, size):
    before, after = (x.shape[:dim], x.shape[dim + 1 :])
    return jnp.moveaxis(x.reshape(*before, size, -1, *after), dim, 0)


def sent_and_summed(x, axis, dim):
    pieces = split_up(x, dim, lax.axis_size(axis))
    arrived = lax.all_to_all(pieces, axis, split_axis=0, concat_axis=0, tiled=True)
    return arrived.astype(jnp.float32).sum(axis=0)


def contract_rows(left, right):
    return lax.dot_general(
        left, right, (((0,), (0,)), ((), ())), preferred_element_type=jnp.float32
    )


def contract_last(left, right):
    return lax.dot_general(
        left, right, (((1,), (1,)), ((), ())), preferred_element_type=jnp.float32
    )


def body(hidden_in, down_weight, keep_mask):
    pruned = down_weight * keep_mask.astype(down_weight.dtype)
    all_features = lax.all_gather(hidden_in, "col", axis=1, tiled=True)
    summed = contract_last(all_features, lax.all_gather(pruned, "tok", axis=1, tiled=True))
    layer_cols = summed.astype(jnp.bfloat16)
    scaling = 2.0 / (layer_cols.shape[0] * lax.axis_size("tok"))
    whole = gathered_copies(layer_cols, "col", 1)
    share_rows = whole.shape[0] // lax.axis_size("col")
    layer_out = lax.dynamic_slice_in_dim(whole, lax.axis_index("col") * share_rows, share_rows, 0)
    hessian_term = contract_rows(layer_cols, whole)
    hessian = sent_and_summed((hessian_term * scaling).astype(jnp.bfloat16), "tok", 1)
    return (layer_out, hessian)


def solution(mesh):
    in_specs = (P("tok", "col"), P("col", "tok"), P("col", "tok"))
    out_specs = (P(("tok", "col"), None), P("col", "tok"))
    return jax.shard_map(body, mesh=mesh, in_specs=in_specs, out_specs=out_specs, check_vma=False)
```

profile of v0, /device:TPU:1, one launch (start us, length us, event | category | flops | bytes accessed | tf_op | source)
XLA Modules:
  0.0 347.3 jit_solution(11855072798509974966)
XLA Ops:
  7.2 0.0 all-gather.3.cloned.1.call-start
  7.2 3.4 convert_multiply_fusion
  10.7 0.0 all-gather.3.cloned.1.call-update
  10.7 0.0 all-gather.5.cloned.1.call-start
  10.7 0.7 all-gather.5.cloned.1.call-update
  11.4 65.1 %all-gather.3.cloned.1.call-done = bf16[144,36864]{1,0:T(8,128)(2,1)} async-done(((bf16[144,4608]{1,0:T(8,128)(2,1)}), bf16[144,36864]{1,0:T(8,128)(2,1)}) %all-gather.3.cloned.1.call-update) | async-done | bytes 10616848 | tf_op jit(solution)/shard_map/all_gather | solution.py:48
  76.6 152.6 %all-gather.5.cloned.1.call-done = bf16[256,36864]{1,0:T(8,128)(2,1)} async-done(((bf16[256,1152]{1,0:T(8,128)(2,1)}), bf16[256,36864]{1,0:T(8,128)(2,1)}) %all-gather.5.cloned.1.call-update) | async-done | bytes 18874384 | tf_op jit(solution)/shard_map/all_gather | solution.py:47
  229.1 12.8 %convolution_convert_fusion = bf16[144,256]{1,0:T(8,128)(2,1)S(1)} fusion(bf16[144,36864]{1,0:T(8,128)(2,1)} %all-gather.3.cloned.1.call-done, bf16[256,36864]{1,0:T(8,128)(2,1)} %all-gather.5.cloned.1.call-done), kind=kOutput, calls=%fused_computation.5 | convolution fusion | flops 2717945856 | bytes 29564928 | tf_op jit(solution)/shard_map/dot_general | solution.py:40
  241.9 0.2 broadcast_in_dim.2
  242.1 58.9 %all_to_all.10 = bf16[32,256,144]{1,2,0:T(8,128)(2,1)S(1)} all-to-all(bf16[32,256,144]{1,2,0:T(8,128)(2,1)S(1)} %broadcast_in_dim.2), channel_id=1, replica_groups=mesh['tok'=8,'col'=32] {'col'}, dimensions={0} | all-to-all | bytes 4718592 | tf_op jit(solution)/shard_map/all_to_all | solution.py:15
  300.9 2.0 fusion
  303.0 3.7 %reshape.12 = bf16[144,8,576]{2,1,0:T(8,128)(2,1)} reshape(bf16[144,4608]{1,0:T(8,128)(2,1)} %fusion) | data formatting | bytes 2654208 | tf_op jit(solution)/shard_map/reshape | solution.py:24
  306.7 2.7 copy.10
  309.4 9.1 %all-to-all-start.1 = ((bf16[8,144,576]{2,1,0:T(8,128)(2,1)}), bf16[8,144,576]{2,1,0:T(8,128)(2,1)}, u32[]{:S(2)}, u32[]{:S(2)}) async-start(bf16[8,144,576]{2,1,0:T(8,128)(2,1)} %bitcast.13), calls=%async_computation.1 | async-start | bytes 2949120 | tf_op jit(solution)/shard_map/all_to_all | solution.py:29
  318.4 0.4 constant_dynamic-slice_fusion
  318.8 1.0 copy.8
  319.8 18.3 %all-to-all-done.1 = bf16[8,144,576]{2,1,0:T(8,128)(2,1)} async-done(((bf16[8,144,576]{2,1,0:T(8,128)(2,1)}), bf16[8,144,576]{2,1,0:T(8,128)(2,1)}, u32[]{:S(2)}, u32[]{:S(2)}) %all-to-all-start.1) | async-done | bytes 1327136 | tf_op jit(solution)/shard_map/all_to_all | solution.py:29
  338.1 2.4 convert_reduce_fusion
Async XLA Ops:
  7.2 69.4 %all-gather.3.cloned.1.call-start = ((), (), s32[]{:S(2)}) async-start(), calls=%async_computation.2 | async-start | bytes 11943936 | tf_op jit(solution)/shard_map/all_gather | solution.py:48
  10.7 218.5 %all-gather.5.cloned.1.call-start = ((), (), s32[]{:S(2)}) async-start(), calls=%async_computation.3 | async-start | bytes 19464192 | tf_op jit(solution)/shard_map/all_gather | solution.py:47
  309.4 28.7 %all-to-all-start.1 = ((bf16[8,144,576]{2,1,0:T(8,128)(2,1)}), bf16[8,144,576]{2,1,0:T(8,128)(2,1)}, u32[]{:S(2)}, u32[]{:S(2)}) async-start(bf16[8,144,576]{2,1,0:T(8,128)(2,1)} %bitcast.13), calls=%async_computation.1 | async-start | bytes 2949120 | tf_op jit(solution)/shard_map/all_to_all | solution.py:29
Sparse Core Ops, SparseCore 0:
  10.8 65.7 all-gather.2
  79.3 149.8 all-gather.4
where the time goes:
time: 348 us; the launch traced here: 347 us
  waiting for transfers between devices  237 us (68%)
  blocking collectives  58.9 us (17%)
  matrix products  14.8 us (4%)
  between operations  14.1 us (4%)
  starting transfers between devices  9.16 us (3%)
  local copies, waits for them, and re-layouts  7.93 us (2%)
  other arithmetic  5.8 us (2%)
    all_gather x1, waiting for transfers between devices, body(): all_features = lax.all_gather(hidden_in, 'col', axis=1, tiled=True)  153 us
    all_gather x1, waiting for transfers between devices, body(): lax.all_gather(pruned, 'tok', axis=1, tiled=True)  65.1 us
    all_to_all x1, blocking collectives, from_everyone(): lax.all_to_all(jnp.broadcast_to(x[None], (size, *x.shape)), axis, 0, 0, t...  58.9 us
    all_to_all x1, waiting for transfers between devices, sent_and_summed(): lax.all_to_all(pieces, axis, split_axis=0, concat_axis=0, tiled=True)  18.3 us
    dot_general x1, matrix products, contract_last(): lax.dot_general(left, right, (((1,), (1,)), ((), ())), preferred_element_...  12.8 us
    all_to_all x1, starting transfers between devices, sent_and_summed(): lax.all_to_all(pieces, axis, split_axis=0, concat_axis=0, tiled=True)  9.08 us
  transfers between devices with their start and end apart: 3, of which 3 were waited for; matrix products, arithmetic and copies ran while one was open for 0% of the time, Pallas kernels for 0%

commit v1 on v0

--- a/solution.py
+++ b/solution.py
@@ -2,6 +2,19 @@
 import jax.numpy as jnp
 from jax import lax
 from jax.sharding import PartitionSpec as P
+
+
+def ring_gather(shard, axis, dim):
+    ways = lax.axis_size(axis)
+    up = [(d, (d + 1) % ways) for d in range(ways)]
+    down = [(d, (d - 1) % ways) for d in range(ways)]
+    earlier, later = ([shard], [shard])
+    for _ in range(ways // 2):
+        earlier.append(lax.ppermute(earlier[-1], axis, up))
+    for _ in range((ways - 1) // 2):
+        later.append(lax.ppermute(later[-1], axis, down))
+    line = jnp.concatenate([*earlier[::-1], *later[1:]], axis=dim)
+    return jnp.roll(line, (lax.axis_index(axis) - ways // 2) * shard.shape[dim], axis=dim)
 
 
 def laid_out(pieces, dim):
@@ -45,7 +58,7 @@
 def body(hidden_in, down_weight, keep_mask):
     pruned = down_weight * keep_mask.astype(down_weight.dtype)
     all_features = lax.all_gather(hidden_in, "col", axis=1, tiled=True)
-    summed = contract_last(all_features, lax.all_gather(pruned, "tok", axis=1, tiled=True))
+    summed = contract_last(all_features, ring_gather(pruned, "tok", 1))
     layer_cols = summed.astype(jnp.bfloat16)
     scaling = 2.0 / (layer_cols.shape[0] * lax.axis_size("tok"))
     whole = gathered_copies(layer_cols, "col", 1)

time: 348 us -> 283 us (0.81)
  waiting for transfers between devices: 237 us -> 123 us
  local copies, waits for them, and re-layouts: 7.93 us -> 38.8 us
  starting transfers between devices: 9.16 us -> 28.7 us
    all_gather x1, waiting for transfers between devices: 153 us -> 53.9 us  [body(): all_features = lax.all_gather(hidden_in, 'col', axis=1, tiled=True)]
    all_gather x1 -> x0, waiting for transfers between devices: 65.1 us -> none  [body(): lax.all_gather(pruned, 'tok', axis=1, tiled=True)]
    ppermute x0 -> x7, waiting for transfers between devices: none -> 49.8 us  [the longest x4 48.5 us: ring_gather(): earlier.append(lax.ppermute(earlier[-1], axis, up))]
    unnamed x1 -> x20, local copies, waits for them, and re-layouts: 0.98 us -> 30.7 us
    ppermute x0 -> x7, starting transfers between devices: none -> 19.5 us  [the longest x4 10.1 us: ring_gather(): earlier.append(lax.ppermute(earlier[-1], axis, up))]
  transfers between devices with their start and end apart: 3 -> 9, of which waited for: 3 -> 8; matrix products, arithmetic and copies ran while one was open for 0% -> 12% of each run, Pallas kernels for 0% -> 0%
where the time goes in v1:
time: 283 us; the launch traced here: 282 us
  waiting for transfers between devices  123 us (43%)
  blocking collectives  58.9 us (21%)
  local copies, waits for them, and re-layouts  38.8 us (14%)
  starting transfers between devices  28.7 us (10%)
  matrix products  14.5 us (5%)
  between operations  14.1 us (5%)
  other arithmetic  4.69 us (2%)
    all_to_all x1, blocking collectives, from_everyone(): lax.all_to_all(jnp.broadcast_to(x[None], (size, *x.shape)), axis, 0, 0, t...  58.9 us
    all_gather x1, waiting for transfers between devices, body(): all_features = lax.all_gather(hidden_in, 'col', axis=1, tiled=True)  53.9 us
    ppermute x4, waiting for transfers between devices, ring_gather(): earlier.append(lax.ppermute(earlier[-1], axis, up))  48.5 us
    unnamed x20, local copies, waits for them, and re-layouts  30.7 us
    all_to_all x1, waiting for transfers between devices, sent_and_summed(): lax.all_to_all(pieces, axis, split_axis=0, concat_axis=0, tiled=True)  18.3 us
    dot_general x1, matrix products, contract_last(): lax.dot_general(left, right, (((1,), (1,)), ((), ())), preferred_element_...  12.6 us
    ppermute x4, starting transfers between devices, ring_gather(): earlier.append(lax.ppermute(earlier[-1], axis, up))  10.1 us
    ppermute x3, starting transfers between devices, ring_gather(): later.append(lax.ppermute(later[-1], axis, down))  9.39 us
  transfers between devices with their start and end apart: 9, of which 8 were waited for; matrix products, arithmetic and copies ran while one was open for 12% of the time, Pallas kernels for 0%

profile of v1, /device:TPU:1, one launch (start us, length us, event | category | flops | bytes accessed | tf_op | source)
XLA Modules:
  0.0 282.3 jit_solution(267600912900387181)
XLA Ops:
  7.2 0.0 all-gather.2.cloned.1.call-start
  7.2 0.7 all-gather.2.cloned.1.call-update
  7.9 2.3 convert_multiply_fusion
  10.2 2.6 collective-permute-start
  12.8 14.7 %collective-permute-done = bf16[144,4608]{1,0:T(8,128)(2,1)S(1)} collective-permute-done((bf16[144,4608]{1,0:T(8,128)(2,1)S(1)}, bf16[144,4608]{1,0:T(8,128)(2,1)S(1)}, u32[]{:S(2)}, u32[]{:S(2)}) %collective-permute-start) | collective-permute-done | bytes 1327136 | tf_op jit(solution)/shard_map/ppermute | solution.py:13
  27.6 2.5 collective-permute-start.1
  30.0 1.8 collective-permute-start.4
  31.9 12.9 %collective-permute-done.1 = bf16[144,4608]{1,0:T(8,128)(2,1)S(1)} collective-permute-done((bf16[144,4608]{1,0:T(8,128)(2,1)S(1)}, bf16[144,4608]{1,0:T(8,128)(2,1)S(1)}, u32[]{:S(2)}, u32[]{:S(2)}) %collective-permute-start.1) | collective-permute-done | bytes 1327136 | tf_op jit(solution)/shard_map/ppermute | solution.py:13
  44.8 0.0 copy-start
  44.8 2.5 collective-permute-start.2
  47.3 0.4 collective-permute-done.4
  47.7 0.0 copy-done
  47.7 3.8 %collective-permute-start.5 = (bf16[144,4608]{1,0:T(8,128)(2,1)}, bf16[144,4608]{1,0:T(8,128)(2,1)}, u32[]{:S(2)}, u32[]{:S(2)}) collective-permute-start(bf16[144,4608]{1,0:T(8,128)(2,1)} %collective-permute-done.4), channel_id=1, source_target_pairs={{0,224},{32,0},{64,32},{96,64},{128,96},{160,128},{192,160},{224,1... | collective-permute-start | bytes 3981320 | tf_op jit(solution)/shard_map/ppermute | solution.py:15
  51.4 10.5 %collective-permute-done.2 = bf16[144,4608]{1,0:T(8,128)(2,1)} collective-permute-done((bf16[144,4608]{1,0:T(8,128)(2,1)S(1)}, bf16[144,4608]{1,0:T(8,128)(2,1)}, u32[]{:S(2)}, u32[]{:S(2)}) %collective-permute-start.2) | collective-permute-done | bytes 1327136 | tf_op jit(solution)/shard_map/ppermute | solution.py:13
  62.0 2.6 collective-permute-start.3
  64.6 0.0 copy-start.1
  64.6 0.9 collective-permute-done.5
  65.5 3.8 %collective-permute-start.6 = (bf16[144,4608]{1,0:T(8,128)(2,1)}, bf16[144,4608]{1,0:T(8,128)(2,1)S(1)}, u32[]{:S(2)}, u32[]{:S(2)}) collective-permute-start(bf16[144,4608]{1,0:T(8,128)(2,1)} %collective-permute-done.5), channel_id=1, source_target_pairs={{0,224},{32,0},{64,32},{96,64},{128,96},{160,128},{192,160},{224,1... | collective-permute-start | bytes 3981320 | tf_op jit(solution)/shard_map/ppermute | solution.py:15
  69.3 10.3 %collective-permute-done.3 = bf16[144,4608]{1,0:T(8,128)(2,1)} collective-permute-done((bf16[144,4608]{1,0:T(8,128)(2,1)}, bf16[144,4608]{1,0:T(8,128)(2,1)}, u32[]{:S(2)}, u32[]{:S(2)}) %collective-permute-start.3) | collective-permute-done | bytes 1327136 | tf_op jit(solution)/shard_map/ppermute | solution.py:13
  79.6 2.5 constant_dynamic-update-slice_fusion.15
  82.1 2.5 constant_dynamic-update-slice_fusion.14
  84.6 2.5 constant_dynamic-update-slice_fusion.13
  87.1 1.2 constant_dynamic-update-slice_fusion.12
  88.2 1.1 constant_dynamic-update-slice_fusion.11
  89.4 2.5 constant_dynamic-update-slice_fusion.10
  91.9 2.5 constant_dynamic-update-slice_fusion.9
  94.4 0.0 collective-permute-done.6
  94.4 1.2 constant_dynamic-update-slice_fusion.8
  95.6 2.5 constant_dynamic-update-slice_fusion.7
  98.1 2.7 constant_dynamic-update-slice_fusion.6
  100.8 0.0 copy-done.1
  100.8 1.2 constant_dynamic-update-slice_fusion.5
  101.9 1.2 constant_dynamic-update-slice_fusion.4
  103.1 1.2 constant_dynamic-update-slice_fusion.3
  104.3 2.5 constant_dynamic-update-slice_fusion.2
  106.8 2.5 constant_dynamic-update-slice_fusion.1
  109.3 1.2 constant_dynamic-update-slice_fusion
  110.5 53.9 %all-gather.2.cloned.1.call-done = bf16[256,36864]{1,0:T(8,128)(2,1)} async-done(((bf16[256,1152]{1,0:T(8,128)(2,1)}), bf16[256,36864]{1,0:T(8,128)(2,1)}) %all-gather.2.cloned.1.call-update) | async-done | bytes 18874384 | tf_op jit(solution)/shard_map/all_gather | solution.py:60
  164.4 12.6 %fusion.3 = bf16[144,256]{1,0:T(8,128)(2,1)S(1)} fusion(bf16[256,36864]{1,0:T(8,128)(2,1)} %all-gather.2.cloned.1.call-done, bf16[144,73728]{1,0:T(8,128)(2,1)} %constant_dynamic-update-slice_fusion, s32[]{:T(128)S(6)} %select_n.17), kind=kOutput, calls=%fused_computation.7 | convolution fusion | flops 2717945856 | bytes 29564932 | tf_op jit(solution)/shard_map/dot_general | solution.py:53
  177.0 0.2 broadcast_in_dim.2
  177.1 58.9 %all_to_all.10 = bf16[32,256,144]{1,2,0:T(8,128)(2,1)S(1)} all-to-all(bf16[32,256,144]{1,2,0:T(8,128)(2,1)S(1)} %broadcast_in_dim.2), channel_id=1, replica_groups=mesh['tok'=8,'col'=32] {'col'}, dimensions={0} | all-to-all | bytes 4718592 | tf_op jit(solution)/shard_map/all_to_all | solution.py:28
  236.0 2.0 fusion.2
  238.0 3.7 %reshape.12 = bf16[144,8,576]{2,1,0:T(8,128)(2,1)} reshape(bf16[144,4608]{1,0:T(8,128)(2,1)} %fusion.2) | data formatting | bytes 2654208 | tf_op jit(solution)/shard_map/reshape | solution.py:37
  241.7 2.7 copy.10
  244.4 9.1 %all-to-all-start.1 = ((bf16[8,144,576]{2,1,0:T(8,128)(2,1)}), bf16[8,144,576]{2,1,0:T(8,128)(2,1)}, u32[]{:S(2)}, u32[]{:S(2)}) async-start(bf16[8,144,576]{2,1,0:T(8,128)(2,1)} %bitcast.12), calls=%async_computation.1 | async-start | bytes 2949120 | tf_op jit(solution)/shard_map/all_to_all | solution.py:42
  253.5 0.4 constant_dynamic-slice_fusion
  253.9 1.0 copy.8
  254.9 18.3 %all-to-all-done.1 = bf16[8,144,576]{2,1,0:T(8,128)(2,1)} async-done(((bf16[8,144,576]{2,1,0:T(8,128)(2,1)}), bf16[8,144,576]{2,1,0:T(8,128)(2,1)}, u32[]{:S(2)}, u32[]{:S(2)}) %all-to-all-start.1) | async-done | bytes 1327136 | tf_op jit(solution)/shard_map/all_to_all | solution.py:42
  273.1 2.4 convert_reduce_fusion
Async XLA Ops:
  7.2 157.2 %all-gather.2.cloned.1.call-start = ((), (), s32[]{:S(2)}) async-start(), calls=%async_computation.2 | async-start | bytes 19464192 | tf_op jit(solution)/shard_map/all_gather | solution.py:60
  10.2 17.3 %collective-permute-start = (bf16[144,4608]{1,0:T(8,128)(2,1)S(1)}, bf16[144,4608]{1,0:T(8,128)(2,1)S(1)}, u32[]{:S(2)}, u32[]{:S(2)}) collective-permute-start(bf16[144,4608]{1,0:T(8,128)(2,1)S(1)} %convert_multiply_fusion), channel_id=1, source_target_pairs={{0,32},{32,64},{64,96},{96,128},{128,160},{160,192},{192,224},{224... | collective-permute-start | bytes 3981320 | tf_op jit(solution)/shard_map/ppermute | solution.py:13
  27.6 17.2 %collective-permute-start.1 = (bf16[144,4608]{1,0:T(8,128)(2,1)S(1)}, bf16[144,4608]{1,0:T(8,128)(2,1)S(1)}, u32[]{:S(2)}, u32[]{:S(2)}) collective-permute-start(bf16[144,4608]{1,0:T(8,128)(2,1)S(1)} %collective-permute-done), channel_id=1, source_target_pairs={{0,32},{32,64},{64,96},{96,128},{128,160},{160,192},{192,224},{224... | collective-permute-start | bytes 3981320 | tf_op jit(solution)/shard_map/ppermute | solution.py:13
  30.0 17.6 %collective-permute-start.4 = (bf16[144,4608]{1,0:T(8,128)(2,1)S(1)}, bf16[144,4608]{1,0:T(8,128)(2,1)}, u32[]{:S(2)}, u32[]{:S(2)}) collective-permute-start(bf16[144,4608]{1,0:T(8,128)(2,1)S(1)} %convert_multiply_fusion), channel_id=1, source_target_pairs={{0,224},{32,0},{64,32},{96,64},{128,96},{160,128},{192,160},{224,1... | collective-permute-start | bytes 3981320 | tf_op jit(solution)/shard_map/ppermute | solution.py:15
  44.8 2.9 %copy-start = (bf16[144,4608]{1,0:T(8,128)(2,1)}, bf16[144,4608]{1,0:T(8,128)(2,1)S(1)}, u32[]{:S(2)}) copy-start(bf16[144,4608]{1,0:T(8,128)(2,1)S(1)} %collective-permute-done.1) | copy-start | bytes 3981316
  44.8 17.2 %collective-permute-start.2 = (bf16[144,4608]{1,0:T(8,128)(2,1)S(1)}, bf16[144,4608]{1,0:T(8,128)(2,1)}, u32[]{:S(2)}, u32[]{:S(2)}) collective-permute-start(bf16[144,4608]{1,0:T(8,128)(2,1)S(1)} %collective-permute-done.1), channel_id=1, source_target_pairs={{0,32},{32,64},{64,96},{96,128},{128,160},{160,192},{192,224},{224... | collective-permute-start | bytes 3981320 | tf_op jit(solution)/shard_map/ppermute | solution.py:13
  47.7 17.8 %collective-permute-start.5 = (bf16[144,4608]{1,0:T(8,128)(2,1)}, bf16[144,4608]{1,0:T(8,128)(2,1)}, u32[]{:S(2)}, u32[]{:S(2)}) collective-permute-start(bf16[144,4608]{1,0:T(8,128)(2,1)} %collective-permute-done.4), channel_id=1, source_target_pairs={{0,224},{32,0},{64,32},{96,64},{128,96},{160,128},{192,160},{224,1... | collective-permute-start | bytes 3981320 | tf_op jit(solution)/shard_map/ppermute | solution.py:15
  62.0 17.6 %collective-permute-start.3 = (bf16[144,4608]{1,0:T(8,128)(2,1)}, bf16[144,4608]{1,0:T(8,128)(2,1)}, u32[]{:S(2)}, u32[]{:S(2)}) collective-permute-start(bf16[144,4608]{1,0:T(8,128)(2,1)} %collective-permute-done.2), channel_id=1, source_target_pairs={{0,32},{32,64},{64,96},{96,128},{128,160},{160,192},{192,224},{224... | collective-permute-start | bytes 3981320 | tf_op jit(solution)/shard_map/ppermute | solution.py:13
  64.6 36.2 %copy-start.1 = (bf16[144,4608]{1,0:T(8,128)(2,1)S(1)}, bf16[144,4608]{1,0:T(8,128)(2,1)}, u32[]{:S(2)}) copy-start(bf16[144,4608]{1,0:T(8,128)(2,1)} %copy-done) | copy-start | bytes 3981316
  65.5 29.0 %collective-permute-start.6 = (bf16[144,4608]{1,0:T(8,128)(2,1)}, bf16[144,4608]{1,0:T(8,128)(2,1)S(1)}, u32[]{:S(2)}, u32[]{:S(2)}) collective-permute-start(bf16[144,4608]{1,0:T(8,128)(2,1)} %collective-permute-done.5), channel_id=1, source_target_pairs={{0,224},{32,0},{64,32},{96,64},{128,96},{160,128},{192,160},{224,1... | collective-permute-start | bytes 3981320 | tf_op jit(solution)/shard_map/ppermute | solution.py:15
  244.4 28.7 %all-to-all-start.1 = ((bf16[8,144,576]{2,1,0:T(8,128)(2,1)}), bf16[8,144,576]{2,1,0:T(8,128)(2,1)}, u32[]{:S(2)}, u32[]{:S(2)}) async-start(bf16[8,144,576]{2,1,0:T(8,128)(2,1)} %bitcast.12), calls=%async_computation.1 | async-start | bytes 2949120 | tf_op jit(solution)/shard_map/all_to_all | solution.py:42
Sparse Core Ops, SparseCore 0:
  10.7 153.6 all-gather.1
